TPU v7x, 512 devices: a whole 4x4x16 slice. The times are simulated.
512 devices in a mesh: hap: 8 (over x, y_lo), snp: 64 (over z, y_hi, core).
Axes of the slice: x: 4, y: 4 (y_hi: 2, y_lo: 2; y = y_hi * 2 + y_lo), z: 16, core: 2. Of those that a mesh axis runs over, the one named last changes fastest.
Arguments:
- packed_panel: int32 [384, 65536], P('hap', 'snp'), may hold values from 0 to 8191, as said below
- components: bfloat16 [64, 4992], P(None, 'hap'), may hold values from -0.078125 to 0.078125
- bounds: int32 [2, 65536], P(None, 'snp'), may hold values from 0 to 65535, as said below
- band_width: int32 [65536], P('snp'), may hold values from 1 to 256
Outputs:
- ld_scores: float32 [65536], P('snp')
Inputs may be any that keep to these rules, and one draw needn't show every extreme that they name: Bit j of packed_panel[w, s] (j from 0 to 12) is the allele of haplotype 13 w + j at SNP s; higher bits are zero. LD blocks are consecutive runs of 1 to 2048 SNPs that cover all SNPs in order; bounds[0, s] and bounds[1, s] are the first and last SNP of the block holding s.
All inputs are finite; a program needn't handle non-finite values.
Results may differ from a plain program's by a relative error of at most 0.00074.
Values may be sent and summed in bfloat16 or wider, within the bound.
A program may use at most 64 MiB of HBM per device.

v0:
```python
import jax
import jax.numpy as jnp
from jax import lax
from jax.sharding import PartitionSpec as P

epsilon = 1e-06


def copy_for_each(array, axis):
    devices = lax.axis_size(axis)
    return lax.all_to_all(
        jnp.broadcast_to(array[None], (devices, *array.shape)), axis, 0, 0, tiled=True
    )


def of_everyone(array, axis):
    everything = copy_for_each(array, axis)
    return jnp.sum(everything, axis=0)


def all_in_one(array, axis):
    leaves = jax.tree.leaves(array)
    turns = sorted(range(len(leaves)), key=lambda k: -leaves[k].size)
    width = (1, *leaves[turns[0]].shape)[-1]
    lines = [
        jnp.pad(leaves[k].reshape(-1), (0, -leaves[k].size % width)).reshape(-1, width)
        for k in turns
    ]
    both, at, found = (copy_for_each(jnp.concatenate(lines), axis), 0, {})
    for k, line in zip(turns, lines):
        piece = both[:, at : at + len(line)].reshape(len(both), -1)
        found[k] = piece[:, : leaves[k].size].reshape(-1, *leaves[k].shape)
        at += len(line)
    numbers = iter(range(len(leaves)))
    return jax.tree.map(lambda _: found[next(numbers)], array)


def folded_in_pairs(pieces, combine):
    while len(jax.tree.leaves(pieces)[0]) > 1:
        pieces = jax.vmap(combine)(
            *(jax.tree.map(lambda part: part[side::2], pieces) for side in (0, 1))
        )
    return jax.tree.map(lambda part: part[0], pieces)


def merged(array, axis, combine):
    pieces = all_in_one(array, axis)
    return folded_in_pairs(pieces, combine)


def padded_2(block, sides, width):
    for axis, dim in sides:
        count = lax.axis_size(axis)
        forward = [(i, i + 1) for i in range(count - 1)]
        backward = [(target, source) for source, target in forward]
        low = lax.ppermute(
            lax.slice_in_dim(block, block.shape[dim] - width, None, axis=dim), axis, forward
        )
        high = lax.ppermute(lax.slice_in_dim(block, 0, width, axis=dim), axis, backward)
        block = jnp.concatenate([low, block, high], axis=dim)
    return block


def unpack(packed):
    shifts = jnp.arange(13, dtype=jnp.int32)
    bit_values = jnp.bitwise_and(jnp.right_shift(packed[:, None, :], shifts[None, :, None]), 1)
    return bit_values.reshape(packed.shape[0] * 13, packed.shape[1]).astype(jnp.bfloat16)


def project(components, packed_panel):
    column_count = packed_panel.shape[1]
    block_size = min(256, column_count)
    zeroed = jnp.zeros((components.shape[0], column_count), jnp.float32)

    def add_block(block_index, accumulated):
        packed = lax.dynamic_slice_in_dim(packed_panel, block_index * block_size, block_size, 1)
        product = jnp.dot(components, unpack(packed), preferred_element_type=jnp.float32)
        return lax.dynamic_update_slice_in_dim(accumulated, product, block_index * block_size, 1)

    return lax.fori_loop(0, column_count // block_size, add_block, zeroed)


def combine_moments(earlier, later):
    left_weight, left_mean, left_spread = earlier
    right_weight, right_mean, right_spread = later
    joined_weight = left_weight + right_weight
    difference = right_mean - left_mean
    joined_mean = left_mean + difference * (right_weight / joined_weight)
    joined_spread = (
        left_spread
        + right_spread
        + difference * difference * (left_weight * right_weight / joined_weight)
    )
    return (joined_weight, joined_mean, joined_spread)


def local_moments(factor):
    local_mean = jnp.mean(factor, axis=1)
    spread = jnp.sum(jnp.square(factor - local_mean[:, None]), axis=1)
    weight = jnp.full((), factor.shape[1], jnp.float32)
    return (weight, local_mean, spread)


def band_scores(padded, inverse, bounds, band_width, offset, start_row, row_count, reach_width):
    component_count = padded.shape[0]
    block_size = min(256, row_count)

    def block_scores(block_index):
        first_row = start_row + block_index * block_size
        row_part = lax.dynamic_slice_in_dim(padded, first_row + reach_width, block_size, 1)
        column_part = lax.dynamic_slice_in_dim(padded, first_row, block_size + 2 * reach_width, 1)
        inverse_rows = lax.dynamic_slice_in_dim(inverse, first_row + reach_width, block_size, 0)
        inverse_columns = lax.dynamic_slice_in_dim(
            inverse, first_row, block_size + 2 * reach_width, 0
        )
        block_first = lax.dynamic_slice_in_dim(bounds[0], first_row, block_size, 0)
        block_last = lax.dynamic_slice_in_dim(bounds[1], first_row, block_size, 0)
        row_reach = lax.dynamic_slice_in_dim(band_width, first_row, block_size, 0)
        inner_products = lax.dot_general(
            row_part, column_part, (((0,), (0,)), ((), ())), preferred_element_type=jnp.float32
        )
        correlation = (
            inner_products
            * (1.0 / component_count)
            * inverse_rows[:, None]
            * inverse_columns[None, :]
        )
        row_position = offset + first_row + jnp.arange(block_size, dtype=jnp.int32)
        column_position = (
            offset
            + first_row
            - reach_width
            + jnp.arange(block_size + 2 * reach_width, dtype=jnp.int32)
        )
        window_low = jnp.maximum(block_first, row_position - row_reach)
        window_high = jnp.minimum(block_last, row_position + row_reach)
        inside = (
            (column_position[None, :] >= window_low[:, None])
            & (column_position[None, :] <= window_high[:, None])
            & (column_position[None, :] != row_position[:, None])
        )
        squared_sum = jnp.sum(jnp.where(inside, correlation * correlation, 0.0), axis=1)
        window_count = jnp.sum(inside.astype(jnp.float32), axis=1)
        return component_count * squared_sum / jnp.maximum(window_count, 1.0)

    blocks = jnp.arange(row_count // block_size, dtype=jnp.int32)
    return lax.map(block_scores, blocks).reshape(row_count)


def on_device(packed_panel, components, bounds, band_width):
    partial_factor = project(components, packed_panel)
    column_count = partial_factor.shape[1]
    factor = of_everyone(partial_factor, "hap")
    weight, average, spread = merged(local_moments(factor), "snp", combine_moments)
    centered = factor - average[:, None]
    normed = (centered * lax.rsqrt(spread / weight + epsilon)[:, None]).astype(jnp.bfloat16)
    reach_width = column_count // 4
    padded = padded_2(normed, (("snp", 1),), reach_width)
    inverse = lax.rsqrt(jnp.mean(jnp.square(padded.astype(jnp.float32)), axis=0) + epsilon)
    offset = lax.axis_index("snp") * column_count
    return band_scores(padded, inverse, bounds, band_width, offset, 0, column_count, reach_width)


def solution(mesh):
    in_specs = (P("hap", "snp"), P(None, "hap"), P(None, "snp"), P("snp"))
    out_specs = P("snp")
    return jax.shard_map(
        on_device, mesh=mesh, in_specs=in_specs, out_specs=out_specs, check_vma=False
    )
```

profile of v0, /device:TPU:1, one launch (start us, length us, event | category | flops | bytes accessed | tf_op | source)
XLA Modules:
  0.0 104.4 jit_solution(16991273546229658975)
XLA Ops:
  0.0 5.9 %while.25 = (s32[]{:T(128)}, f32[64,1024]{1,0:T(8,128)S(1)}, s32[48,1024]{1,0:T(8,128)}, bf16[64,624]{1,0:T(8,128)(2,1)}, s32[]{:T(128)}, /*index=5*/s32[]{:T(128)}, s32[]{:T(128)}, s32[]{:T(128)}) while((s32[]{:T(128)}, f32[64,1024]{1,0:T(8,128)S(1)}, s32[48,1024]{1,0:T(8,128)}, bf16[64,624]{1,0:T(8,128)(2,1)}, s32[]{:T(128)}, ...), condition=%wide.region_1.0_spmd, body=%wide.region_0.0_spmd.sunk | while | flops 20926468 | bytes 3182055 | solution.py:80
  0.1 0.8 constant_dynamic-slice_fusion.6
  1.0 0.1 shift_right_arithmetic.51
  1.1 0.1 shift_right_arithmetic.53
  1.2 0.3 fusion.30
  1.5 0.8 constant_dynamic-slice_fusion.6
  2.4 0.1 shift_right_arithmetic.51
  2.5 0.1 shift_right_arithmetic.53
  2.7 0.3 fusion.30
  3.0 0.8 constant_dynamic-slice_fusion.6
  3.9 0.1 shift_right_arithmetic.51
  4.0 0.1 shift_right_arithmetic.53
  4.1 0.3 fusion.30
  4.5 0.8 constant_dynamic-slice_fusion.6
  5.4 0.1 shift_right_arithmetic.51
  5.5 0.1 shift_right_arithmetic.53
  5.6 0.3 fusion.30
  5.9 0.2 broadcast_in_dim.23
  6.2 28.7 %all_to_all.10 = f32[8,64,1024]{2,1,0:T(8,128)S(1)} all-to-all(f32[8,64,1024]{2,1,0:T(8,128)S(1)} %broadcast_in_dim.23), channel_id=1, replica_groups=mesh['hap'=8,'snp'=64] {'hap'}, dimensions={0} | all-to-all | bytes 4194304 | tf_op jit(solution)/shard_map/all_to_all | solution.py:11
  34.8 0.3 fusion.12
  35.2 0.2 multiply_reduce_fusion.1
  35.3 0.1 copy-done.2
  35.5 0.1 reshape.130
  35.7 38.3 %all_to_all.11 = f32[64,1,192]{2,1,0:T(1,128)S(1)} all-to-all(f32[64,1,192]{2,1,0:T(1,128)S(1)} %reshape.130), channel_id=1, replica_groups=mesh['hap'=8,'snp'=64] {'snp'}, dimensions={0} | all-to-all | bytes 98304 | tf_op jit(solution)/shard_map/all_to_all | solution.py:11
  73.9 0.5 broadcast.120
  74.4 0.8 reduce.3
  75.2 0.1 reshape.131
  75.4 0.1 slice_reduce_fusion
  75.5 0.1 slice.149
  75.7 0.1 slice.150
  75.8 0.1 slice.153
  75.9 0.1 slice.154
  76.0 0.1 slice.157
  76.1 0.1 slice.158
  76.2 0.1 slice.161
  76.3 0.1 slice.162
  76.4 0.1 slice.165
  76.5 0.1 slice.166
  76.6 0.6 fusion.21
  79.9 0.1 multiply_add_fusion.1
  80.0 0.1 multiply_add_fusion.3
  81.2 0.1 multiply_add_fusion.9
  81.3 0.1 multiply_convert_fusion
  81.4 3.0 %collective-permute-start = (bf16[64,256]{1,0:T(8,128)(2,1)S(1)}, bf16[64,256]{1,0:T(8,128)(2,1)S(1)}, u32[]{:S(2)}, u32[]{:S(2)}) collective-permute-start(bf16[64,256]{1,0:T(8,128)(2,1)S(1)} %get-tuple-element.231), channel_id=1, source_target_pairs={{0,1},{1,2},{2,3},{3,4},{4,5},{5,6},{6,7},{7,8},{8,9},{9,10},{10,1... | collective-permute-start | bytes 98312 | tf_op jit(solution)/shard_map/ppermute | solution.py:56
  84.4 1.9 %collective-permute-start.1 = (bf16[64,256]{1,0:T(8,128)(2,1)S(1)}, bf16[64,256]{1,0:T(8,128)(2,1)S(1)}, u32[]{:S(2)}, u32[]{:S(2)}) collective-permute-start(bf16[64,256]{1,0:T(8,128)(2,1)S(1)} %get-tuple-element.232), channel_id=1, source_target_pairs={{1,0},{2,1},{3,2},{4,3},{5,4},{6,5},{7,6},{8,7},{9,8},{10,9},{11,1... | collective-permute-start | bytes 98312 | tf_op jit(solution)/shard_map/ppermute | solution.py:59
  86.3 4.8 %collective-permute-done.1 = bf16[64,256]{1,0:T(8,128)(2,1)S(1)} collective-permute-done((bf16[64,256]{1,0:T(8,128)(2,1)S(1)}, bf16[64,256]{1,0:T(8,128)(2,1)S(1)}, u32[]{:S(2)}, u32[]{:S(2)}) %collective-permute-start.1) | collective-permute-done | bytes 32800 | tf_op jit(solution)/shard_map/ppermute | solution.py:59
  91.2 12.6 %while.26 = (s32[]{:T(128)}, f32[4,256]{1,0:T(4,128)S(1)}, s32[4]{0:T(128)S(1)}, s32[]{:T(128)}, s32[2,1024]{1,0:T(2,128)S(1)}, /*index=5*/s32[1024]{0:T(1024)},...) while((s32[]{:T(128)}, f32[4,256]{1,0:T(4,128)S(1)}, ...), condition=%wide.region_9.10_spmd, body=%wide.region_6.9_spmd.sunk | while | flops 28510732 | bytes 194902 | solution.py:147
  91.2 0.6 dynamic_slice.80
  92.5 0.8 subtract_maximum_fusion.2
  93.4 0.5 fusion.34
  94.0 0.3 convert_reduce_fusion.2
  94.4 0.6 dynamic_slice.80
  95.7 0.8 subtract_maximum_fusion.2
  96.6 0.5 fusion.34
  97.1 0.3 convert_reduce_fusion.2
  97.5 0.6 dynamic_slice.80
  98.8 0.8 subtract_maximum_fusion.2
  99.7 0.5 fusion.34
  100.3 0.3 convert_reduce_fusion.2
  100.7 0.6 dynamic_slice.80
  102.0 0.8 subtract_maximum_fusion.2
  102.9 0.5 fusion.34
  103.4 0.3 convert_reduce_fusion.2
  103.8 0.6 copy.8
  (95 shorter events, 2.0 us)
Async XLA Ops:
  0.0 1.1 %copy-start = (bf16[64,624]{1,0:T(8,128)(2,1)S(1)}, bf16[64,624]{1,0:T(8,128)(2,1)}, u32[]{:S(2)}) copy-start(bf16[64,624]{1,0:T(8,128)(2,1)} %get-tuple-element.355) | copy-start | bytes 239620 | tf_op jit(solution)/shard_map/while
  1.5 1.1 %copy-start = (bf16[64,624]{1,0:T(8,128)(2,1)S(1)}, bf16[64,624]{1,0:T(8,128)(2,1)}, u32[]{:S(2)}) copy-start(bf16[64,624]{1,0:T(8,128)(2,1)} %get-tuple-element.355) | copy-start | bytes 239620 | tf_op jit(solution)/shard_map/while
  3.0 1.1 %copy-start = (bf16[64,624]{1,0:T(8,128)(2,1)S(1)}, bf16[64,624]{1,0:T(8,128)(2,1)}, u32[]{:S(2)}) copy-start(bf16[64,624]{1,0:T(8,128)(2,1)} %get-tuple-element.355) | copy-start | bytes 239620 | tf_op jit(solution)/shard_map/while
  4.4 1.1 %copy-start = (bf16[64,624]{1,0:T(8,128)(2,1)S(1)}, bf16[64,624]{1,0:T(8,128)(2,1)}, u32[]{:S(2)}) copy-start(bf16[64,624]{1,0:T(8,128)(2,1)} %get-tuple-element.355) | copy-start | bytes 239620 | tf_op jit(solution)/shard_map/while
  34.8 0.7 copy-start.2
  34.8 56.4 %copy-start.1 = (s32[2,1024]{1,0:T(2,128)S(1)}, s32[2,1024]{1,0:T(2,128)}, u32[]{:S(2)}) copy-start(s32[2,1024]{1,0:T(2,128)} %param.10) | copy-start | bytes 24580
  81.4 4.9 %collective-permute-start = (bf16[64,256]{1,0:T(8,128)(2,1)S(1)}, bf16[64,256]{1,0:T(8,128)(2,1)S(1)}, u32[]{:S(2)}, u32[]{:S(2)}) collective-permute-start(bf16[64,256]{1,0:T(8,128)(2,1)S(1)} %get-tuple-element.231), channel_id=1, source_target_pairs={{0,1},{1,2},{2,3},{3,4},{4,5},{5,6},{6,7},{7,8},{8,9},{9,10},{10,1... | collective-permute-start | bytes 98312 | tf_op jit(solution)/shard_map/ppermute | solution.py:56
  84.4 6.7 %collective-permute-start.1 = (bf16[64,256]{1,0:T(8,128)(2,1)S(1)}, bf16[64,256]{1,0:T(8,128)(2,1)S(1)}, u32[]{:S(2)}, u32[]{:S(2)}) collective-permute-start(bf16[64,256]{1,0:T(8,128)(2,1)S(1)} %get-tuple-element.232), channel_id=1, source_target_pairs={{1,0},{2,1},{3,2},{4,3},{5,4},{6,5},{7,6},{8,7},{9,8},{10,9},{11,1... | collective-permute-start | bytes 98312 | tf_op jit(solution)/shard_map/ppermute | solution.py:59
where the time goes:
time: 105 us; the launch traced here: 104 us
  blocking collectives  66.9 us (64%)
  local copies, waits for them, and re-layouts  11.4 us (11%)
  other arithmetic  6.72 us (6%)
  starting transfers between devices  4.88 us (5%)
  waiting for transfers between devices  4.79 us (5%)
  between operations  3.44 us (3%)
  matrix products  3.29 us (3%)
  loops' own time  2.96 us (3%)
    all_to_all x2, blocking collectives, copy_for_each(): lax.all_to_all(jnp.broadcast_to(array[None], (devices, *array.shape)), ax...  66.9 us
    ppermute x1, waiting for transfers between devices, padded_2(): lax.ppermute(lax.slice_in_dim(block, 0, width, axis=dim), axis, backward)  4.79 us
    dynamic_slice x4, local copies, waits for them, and re-layouts, add_block(): lax.dynamic_slice_in_dim(packed_panel, block_index * block_size, block_si...  3.36 us
    max x4, other arithmetic, block_scores(): window_low = jnp.maximum(block_first, row_position - row_reach)  3.08 us
    ppermute x1, starting transfers between devices, padded_2(): lax.ppermute(lax.slice_in_dim(block, block.shape[dim] - width, None, axis...  2.95 us
    another operation x1, loops' own time, band_scores(): return lax.map(block_scores, blocks).reshape(row_count)  2.67 us
    dynamic_slice x4, local copies, waits for them, and re-layouts, band_scores(): return lax.map(block_scores, blocks).reshape(row_count)  2.47 us
    dot_general x4, matrix products, block_scores(): lax.dot_general(row_part, column_part, (((0,), (0,)), ((), ())), preferre...  2.13 us
  transfers between devices with their start and end apart: 2, of which 1 were waited for; matrix products, arithmetic and copies ran while one was open for 0% of the time, Pallas kernels for 0%

commit v1 on v0

v1 whole, which is shorter than its diff:
```python
import functools

import jax
import jax.numpy as jnp
from jax import lax
from jax.experimental import pallas as pl
from jax.experimental.pallas import tpu as pltpu
from jax.sharding import PartitionSpec as P

EPS = 1e-06
K = 64
BITS = 13
PIECE = 128
REACH = 2
WINDOW = 2 * REACH + 1
PLANE = 4
MESH = pl.DeviceIdType.MESH


def ring(value, size):
    return lax.rem(value, size)


def kernel(
    haps, snps, panel, comp, bounds, width, out,
    comp_pad, part, recv, full, normed, weight, masks, scale, near, far,
    part_send, part_recv, full_send, full_recv, halo_send, halo_recv,
    near_send, near_recv, far_send, far_recv,
):
    h, s = lax.axis_index("hap"), lax.axis_index("snp")
    z, sub = lax.div(s, PLANE), lax.rem(s, PLANE)
    planes, plane_size = snps // PLANE, haps * PLANE
    me = h * PLANE + sub
    words, columns = panel.shape
    pieces = columns // PIECE
    left, right = ring(s + snps - 1, snps), ring(s + 1, snps)

    def in_plane(r):
        q = ring(me + r, plane_size)
        return (lax.div(q, PLANE), z * PLANE + lax.rem(q, PLANE))

    def along_z(r):
        return (h, ring(z + r, planes) * PLANE + sub)

    barrier = pltpu.get_barrier_semaphore()

    def greet(device):
        pl.semaphore_signal(barrier, inc=1, device_id=device, device_id_type=MESH)

    @pl.loop(1, plane_size)
    def _(r):
        greet(in_plane(r))

    @pl.loop(1, planes)
    def _(r):
        greet(along_z(r))

    greet((h, left))
    greet((h, right))

    depth = comp_pad.shape[1]
    comp_pad[...] = jnp.zeros_like(comp_pad)
    comp_pad[:, : comp.shape[1]] = comp[...]
    col = lax.broadcasted_iota(jnp.int32, (8, depth), 1)
    bit = jnp.zeros_like(col)
    for j in range(1, BITS + 1):
        bit = bit + (col >= j * words).astype(jnp.int32)
    source = jnp.where(col < words * BITS, BITS * (col - words * bit) + bit, -1)[:1]
    level = (jnp.right_shift(1 << (BITS - 1), bit).astype(jnp.float32) * (0.5 ** (BITS - 1)))[:1]
    row = lax.broadcasted_iota(jnp.int32, (depth, depth), 0)
    chosen = jnp.where(row == source, level, 0.0).astype(jnp.bfloat16)
    mixed = jnp.dot(comp_pad[...], chosen, preferred_element_type=jnp.float32).astype(jnp.bfloat16)

    def project(block):
        at = pl.multiple_of(block * (2 * PIECE), 2 * PIECE)
        packed = panel[:, pl.ds(at, 2 * PIECE)]
        alleles = [
            jnp.bitwise_and(packed, 1 << j).astype(jnp.float32).astype(jnp.bfloat16)
            for j in range(BITS)
        ]
        rest = depth - BITS * words
        alleles.append(jnp.zeros((rest, 2 * PIECE), jnp.bfloat16))
        product = jnp.dot(
            mixed, jnp.concatenate(alleles, axis=0), preferred_element_type=jnp.float32
        )
        part[2 * block] = product[:, :PIECE]
        part[2 * block + 1] = product[:, PIECE:]

    def send_part(to):
        return pltpu.make_async_remote_copy(
            part.at[to], recv.at[h], part_send, part_recv, device_id=(to, s), device_id_type=MESH
        )

    blocks = pieces // 2
    mine, side = lax.div(h, 2), lax.rem(h, 2)
    order = sorted(range(blocks), key=lambda d: (-min(d, blocks - d), d))
    for turn, d in enumerate(order):
        block = ring(mine + d, blocks)
        project(block)
        if turn == 0:
            pl.semaphore_wait(barrier, plane_size + planes)
        if d:
            send_part(2 * block + side).start()
            send_part(2 * block + 1 - side).start()
        else:
            send_part(2 * block + 1 - side).start()
    recv[h] = part[h]

    def wait_for(ref, sem):
        pltpu.make_async_copy(ref, ref, sem).wait()

    wait_for(recv.at[pl.ds(0, pieces - 1)], part_recv)
    total = recv[0]
    for k in range(1, pieces):
        total = total + recv[k]
    full[REACH + h] = total

    lane = lax.broadcasted_iota(jnp.int32, (1, 2 * K), 1)
    first = lane < K
    both = jnp.concatenate([total, total], axis=0).T
    average = jnp.sum(both, axis=0, keepdims=True) * (1.0 / PIECE)
    off = both - average
    spread = jnp.sum(off * off, axis=0, keepdims=True)
    near[me] = jnp.where(first, average, spread)

    def send_near(r):
        return pltpu.make_async_remote_copy(
            near.at[me], near.at[me], near_send, near_recv,
            device_id=in_plane(r), device_id_type=MESH,
        )

    @pl.loop(1, plane_size)
    def _(r):
        send_near(r).start()

    def send_full(r):
        to = ring(h + r, haps)
        return pltpu.make_async_remote_copy(
            full.at[REACH + h], full.at[REACH + h], full_send, full_recv,
            device_id=(to, s), device_id_type=MESH,
        )

    for r in range(1, haps):
        send_full(r).start()

    def merge(ref, count, weight_each):
        rows = [ref[k] for k in range(count)]
        summed = functools.reduce(jnp.add, rows)
        mean = summed * (1.0 / count)
        offs = [r - mean for r in rows]
        between = functools.reduce(jnp.add, [o * o for o in offs]) * weight_each
        return mean, summed, between

    position = lax.broadcasted_iota(jnp.int32, (1, PIECE), 1)
    lane_at = lax.broadcasted_iota(jnp.int32, (PIECE, PIECE), 1)
    row_at = lax.broadcasted_iota(jnp.int32, (PIECE, PIECE), 0)

    def windows(b):
        at = s * columns + b * PIECE
        here = position + at
        reach = width[b : b + 1, :]
        cut = slice(b * PIECE, (b + 1) * PIECE)
        low = jnp.maximum(bounds[0:1, cut], here - reach)
        high = jnp.minimum(bounds[1:2, cut], here + reach)
        count = (high - low).astype(jnp.float32)
        scale[b : b + 1, :] = (1.0 / K) / jnp.maximum(count, 1.0)
        start = at - REACH * PIECE
        low_rows = jnp.broadcast_to((low - start).astype(jnp.float32), (PIECE, PIECE)).T
        high_rows = jnp.broadcast_to((high - start).astype(jnp.float32), (PIECE, PIECE)).T
        for t in range(WINDOW):
            there = (lane_at + t * PIECE).astype(jnp.float32)
            inside = (there >= low_rows) & (there <= high_rows)
            if t == REACH:
                inside = inside & (lane_at != row_at)
            masks[b, :, t * PIECE : (t + 1) * PIECE] = inside.astype(jnp.float32)

    for b in range(pieces):
        windows(b)

    wait_for(near.at[pl.ds(0, plane_size - 1)], near_recv)
    mean, summed, between = merge(near, plane_size, float(PIECE))
    moved = pltpu.roll(jnp.broadcast_to(between, (8, 2 * K)), K, 1)[:1]
    far[z] = jnp.where(first, mean, summed + moved)

    def send_far(r):
        return pltpu.make_async_remote_copy(
            far.at[z], far.at[z], far_send, far_recv, device_id=along_z(r), device_id_type=MESH
        )

    @pl.loop(1, planes)
    def _(r):
        send_far(r).start()

    wait_for(full.at[pl.ds(REACH, haps - 1)], full_recv)
    low_halo = pltpu.make_async_remote_copy(
        full.at[pl.ds(pieces, REACH)], full.at[pl.ds(0, REACH)],
        halo_send.at[0], halo_recv.at[0], device_id=(h, right), device_id_type=MESH,
    )
    high_halo = pltpu.make_async_remote_copy(
        full.at[pl.ds(REACH, REACH)], full.at[pl.ds(REACH + pieces, REACH)],
        halo_send.at[1], halo_recv.at[1], device_id=(h, left), device_id_type=MESH,
    )
    low_halo.start()
    high_halo.start()
    low_halo.wait_recv()
    high_halo.wait_recv()

    wait_for(far.at[pl.ds(0, planes - 1)], far_recv)
    mean, summed, between = merge(far, planes, float(PIECE * plane_size))
    top = jnp.broadcast_to(jnp.where(first, mean, summed), (2 * K, 2 * K)).T
    between = jnp.broadcast_to(between, (2 * K, 2 * K)).T
    average = top[:K]
    variance = (top[K:] + between[:K]) * (1.0 / (PIECE * plane_size * planes))
    factor = lax.rsqrt(variance + EPS)
    for p in range(pieces + 2 * REACH):
        cut = slice(p * PIECE, (p + 1) * PIECE)
        scaled = ((full[p] - average) * factor).astype(jnp.bfloat16)
        normed[:, cut] = scaled
        wide = scaled.astype(jnp.float32)
        square = jnp.sum(wide * wide, axis=0, keepdims=True)
        weight[:, cut] = 1.0 / (square * (1.0 / K) + EPS)

    for b in range(pieces):
        rows = normed[:, (b + REACH) * PIECE : (b + REACH + 1) * PIECE]
        span = slice(b * PIECE, (b + WINDOW) * PIECE)
        inner = lax.dot_general(
            rows, normed[:, span], (((0,), (0,)), ((), ())), preferred_element_type=jnp.float32
        )
        terms = inner * inner * masks[b] * weight[:, span]
        summed = terms[:, :PIECE]
        for t in range(1, WINDOW):
            summed = summed + terms[:, t * PIECE : (t + 1) * PIECE]
        line = jnp.sum(summed.T, axis=0, keepdims=True)
        own = weight[:, (b + REACH) * PIECE : (b + REACH + 1) * PIECE]
        out[b : b + 1, :] = line * own * scale[b : b + 1, :]

    wait_for(part.at[pl.ds(0, pieces - 1)], part_send)
    wait_for(full.at[pl.ds(0, pieces - 1)], full_send)
    wait_for(near.at[pl.ds(0, plane_size - 1)], near_send)
    wait_for(far.at[pl.ds(0, planes - 1)], far_send)
    low_halo.wait_send()
    high_halo.wait_send()


def on_device(packed_panel, components, bounds, band_width):
    haps, snps = lax.axis_size("hap"), lax.axis_size("snp")
    words, columns = packed_panel.shape
    pieces = columns // PIECE
    depth = -(-words * BITS // PIECE) * PIECE
    plane_size, planes = haps * PLANE, snps // PLANE
    extended = pieces + 2 * REACH
    dma = pltpu.SemaphoreType.DMA
    out = pl.pallas_call(
        functools.partial(kernel, haps, snps),
        out_shape=jax.ShapeDtypeStruct((pieces, PIECE), jnp.float32),
        in_specs=[pl.BlockSpec(memory_space=pltpu.VMEM)] * 4,
        out_specs=pl.BlockSpec(memory_space=pltpu.VMEM),
        scratch_shapes=[
            pltpu.VMEM((K, depth), jnp.bfloat16),
            pltpu.VMEM((pieces, K, PIECE), jnp.float32),
            pltpu.VMEM((pieces, K, PIECE), jnp.float32),
            pltpu.VMEM((extended, K, PIECE), jnp.float32),
            pltpu.VMEM((K, extended * PIECE), jnp.bfloat16),
            pltpu.VMEM((1, extended * PIECE), jnp.float32),
            pltpu.VMEM((pieces, PIECE, WINDOW * PIECE), jnp.float32),
            pltpu.VMEM((pieces, PIECE), jnp.float32),
            pltpu.VMEM((plane_size, 1, 2 * K), jnp.float32),
            pltpu.VMEM((planes, 1, 2 * K), jnp.float32),
            dma, dma, dma, dma, dma((2,)), dma((2,)), dma, dma, dma, dma,
        ],
        compiler_params=pltpu.CompilerParams(collective_id=0, has_side_effects=True),
    )(packed_panel, components, bounds, band_width.reshape(pieces, PIECE))
    return out.reshape(columns)


def solution(mesh):
    return jax.shard_map(
        on_device,
        mesh=mesh,
        in_specs=(P("hap", "snp"), P(None, "hap"), P(None, "snp"), P("snp")),
        out_specs=P("snp"),
        check_vma=False,
    )
```

time: 105 us -> 37.4 us (0.36)
  blocking collectives: 66.9 us -> 0 us
  Pallas kernels: 0 us -> 35.9 us
  local copies, waits for them, and re-layouts: 11.4 us -> 1.28 us
  other arithmetic: 6.72 us -> 0 us
  starting transfers between devices: 4.88 us -> 0 us
  waiting for transfers between devices: 4.79 us -> 0 us
  between operations: 3.44 us -> 0.01 us
  matrix products: 3.29 us -> 0 us
  loops' own time: 2.96 us -> 0 us
    all_to_all x2 -> x0, blocking collectives: 66.9 us -> none  [copy_for_each(): lax.all_to_all(jnp.broadcast_to(array[None], (devices, *array.shape)), ax...]
    pallas_call x0 -> x1, Pallas kernels: none -> 35.9 us  [on_device(): pl.pallas_call(functools.partial(kernel, haps, snps), out_shape=jax.Shape...]
    dynamic_slice x20 -> x0, local copies, waits for them, and re-layouts: 6.2 us -> none  [the longest x4 3.36 us: add_block(): lax.dynamic_slice_in_dim(packed_panel, block_index * block_size, block_si...]
    ppermute x2 -> x0, starting transfers between devices: 4.88 us -> none  [the longest x1 2.95 us: padded_2(): lax.ppermute(lax.slice_in_dim(block, block.shape[dim] - width, None, axis...]
    ppermute x2 -> x0, waiting for transfers between devices: 4.79 us -> none  [the longest x1 4.79 us: padded_2(): lax.ppermute(lax.slice_in_dim(block, 0, width, axis=dim), axis, backward)]
    dot_general x8 -> x0, matrix products: 3.29 us -> none  [the longest x4 2.13 us: block_scores(): lax.dot_general(row_part, column_part, (((0,), (0,)), ((), ())), preferre...]
    max x4 -> x0, other arithmetic: 3.08 us -> none  [block_scores(): window_low = jnp.maximum(block_first, row_position - row_reach)]
    another operation x2 -> x0, loops' own time: 2.96 us -> none  [the longest x1 2.67 us: band_scores(): return lax.map(block_scores, blocks).reshape(row_count)]
  transfers between devices with their start and end apart: 2 -> 0, of which waited for: 1 -> 0; matrix products, arithmetic and copies ran while one was open for 0% -> 0% of each run, Pallas kernels for 0% -> 0%
where the time goes in v1:
time: 37.4 us; the launch traced here: 37.2 us
  Pallas kernels  35.9 us (96%)
  local copies, waits for them, and re-layouts  1.28 us (3%)
    pallas_call x1, Pallas kernels, on_device(): pl.pallas_call(functools.partial(kernel, haps, snps), out_shape=jax.Shape...  35.9 us
    unnamed x1, local copies, waits for them, and re-layouts  1.28 us

profile of v1, /device:TPU:1, one launch (start us, length us, event | category | flops | bytes accessed | tf_op | source)
XLA Modules:
  0.0 37.2 jit_solution(4835761630609824288)
XLA Ops:
  0.0 35.9 %shard_map.46 = f32[8,128]{1,0:T(8,128)} custom-call(s32[48,1024]{1,0:T(8,128)} %panel.1, bf16[64,624]{1,0:T(8,128)(2,1)} %comp.1, s32[2,1024]{1,0:T(2,128)} %bounds.1, s32[8,128]{1,0:T(8,128)} %bitcast.3), custom_call_target="tpu_custom_call" | custom-call | tf_op jit(solution)/shard_map/pallas_call | solution.py:253
  36.0 1.3 %copy.6 = f32[1024]{0:T(1024)} copy(f32[1024]{0:T(1024)} %bitcast.2) | data formatting | bytes 8192

commit v2 on v1

--- a/solution.py
+++ b/solution.py
@@ -22,10 +22,10 @@
 
 
 def kernel(
-    haps, snps, panel, comp, bounds, width, out,
-    comp_pad, part, recv, full, normed, weight, masks, scale, near, far,
+    haps, snps, panel_in, comp_in, bounds_in, width_in, out,
+    panel, comp, bounds, width, comp_pad, part, recv, full, normed, weight, masks, scale, near, far,
     part_send, part_recv, full_send, full_recv, halo_send, halo_recv,
-    near_send, near_recv, far_send, far_recv,
+    near_send, near_recv, far_send, far_recv, panel_sem, input_sem, ready,
 ):
     h, s = lax.axis_index("hap"), lax.axis_index("snp")
     z, sub = lax.div(s, PLANE), lax.rem(s, PLANE)
@@ -42,25 +42,39 @@
     def along_z(r):
         return (h, ring(z + r, planes) * PLANE + sub)
 
+    blocks = pieces // 2
+    mine, side = lax.div(h, 2), lax.rem(h, 2)
+    order = sorted(range(blocks), key=lambda d: (-min(d, blocks - d), d))
+
+    def fetch(turn):
+        at = pl.multiple_of(ring(mine + order[turn], blocks) * (2 * PIECE), 2 * PIECE)
+        cut = pl.ds(at, 2 * PIECE)
+        return pltpu.make_async_copy(panel_in.at[:, cut], panel.at[:, cut], panel_sem.at[turn])
+
+    inputs = [
+        pltpu.make_async_copy(comp_in, comp, input_sem.at[0]),
+        pltpu.make_async_copy(bounds_in, bounds, input_sem.at[1]),
+        pltpu.make_async_copy(width_in, width, input_sem.at[2]),
+    ]
+    inputs[0].start()
+    for turn in range(blocks):
+        fetch(turn).start()
+    inputs[1].start()
+    inputs[2].start()
+
     barrier = pltpu.get_barrier_semaphore()
 
-    def greet(device):
-        pl.semaphore_signal(barrier, inc=1, device_id=device, device_id_type=MESH)
-
-    @pl.loop(1, plane_size)
-    def _(r):
-        greet(in_plane(r))
-
-    @pl.loop(1, planes)
-    def _(r):
-        greet(along_z(r))
-
-    greet((h, left))
-    greet((h, right))
+    def signal(sem, device):
+        pl.semaphore_signal(sem, inc=1, device_id=device, device_id_type=MESH)
+
+    for r in range(1, haps):
+        signal(barrier, (ring(h + r, haps), s))
+    for r in range(1, PLANE):
+        signal(barrier, (h, z * PLANE + ring(sub + r, PLANE)))
+    signal(barrier, along_z(1))
+    signal(barrier, along_z(planes - 1))
 
     depth = comp_pad.shape[1]
-    comp_pad[...] = jnp.zeros_like(comp_pad)
-    comp_pad[:, : comp.shape[1]] = comp[...]
     col = lax.broadcasted_iota(jnp.int32, (8, depth), 1)
     bit = jnp.zeros_like(col)
     for j in range(1, BITS + 1):
@@ -69,6 +83,9 @@
     level = (jnp.right_shift(1 << (BITS - 1), bit).astype(jnp.float32) * (0.5 ** (BITS - 1)))[:1]
     row = lax.broadcasted_iota(jnp.int32, (depth, depth), 0)
     chosen = jnp.where(row == source, level, 0.0).astype(jnp.bfloat16)
+    comp_pad[...] = jnp.zeros_like(comp_pad)
+    inputs[0].wait()
+    comp_pad[:, : comp.shape[1]] = comp[...]
     mixed = jnp.dot(comp_pad[...], chosen, preferred_element_type=jnp.float32).astype(jnp.bfloat16)
 
     def project(block):
@@ -91,20 +108,32 @@
             part.at[to], recv.at[h], part_send, part_recv, device_id=(to, s), device_id_type=MESH
         )
 
-    blocks = pieces // 2
-    mine, side = lax.div(h, 2), lax.rem(h, 2)
-    order = sorted(range(blocks), key=lambda d: (-min(d, blocks - d), d))
+    rounds = [1 << k for k in range(8) if (2 << k) <= planes // 2]
+
+    def tell(k):
+        if k < len(rounds):
+            signal(ready.at[k], along_z(rounds[k]))
+            signal(ready.at[k], along_z(planes - rounds[k]))
+
+    def hear(k):
+        if k < len(rounds):
+            pl.semaphore_wait(ready.at[k], 2)
+
     for turn, d in enumerate(order):
         block = ring(mine + d, blocks)
+        fetch(turn).wait()
         project(block)
         if turn == 0:
-            pl.semaphore_wait(barrier, plane_size + planes)
+            pl.semaphore_wait(barrier, haps + PLANE)
+            tell(0)
         if d:
             send_part(2 * block + side).start()
             send_part(2 * block + 1 - side).start()
         else:
             send_part(2 * block + 1 - side).start()
     recv[h] = part[h]
+    hear(0)
+    tell(1)
 
     def wait_for(ref, sem):
         pltpu.make_async_copy(ref, ref, sem).wait()
@@ -142,6 +171,9 @@
 
     for r in range(1, haps):
         send_full(r).start()
+
+    hear(1)
+    tell(2)
 
     def merge(ref, count, weight_each):
         rows = [ref[k] for k in range(count)]
@@ -174,6 +206,8 @@
                 inside = inside & (lane_at != row_at)
             masks[b, :, t * PIECE : (t + 1) * PIECE] = inside.astype(jnp.float32)
 
+    inputs[1].wait()
+    inputs[2].wait()
     for b in range(pieces):
         windows(b)
 
@@ -187,6 +221,7 @@
             far.at[z], far.at[z], far_send, far_recv, device_id=along_z(r), device_id_type=MESH
         )
 
+    hear(2)
     @pl.loop(1, planes)
     def _(r):
         send_far(r).start()
@@ -253,9 +288,13 @@
     out = pl.pallas_call(
         functools.partial(kernel, haps, snps),
         out_shape=jax.ShapeDtypeStruct((pieces, PIECE), jnp.float32),
-        in_specs=[pl.BlockSpec(memory_space=pltpu.VMEM)] * 4,
+        in_specs=[pl.BlockSpec(memory_space=pltpu.HBM)] * 4,
         out_specs=pl.BlockSpec(memory_space=pltpu.VMEM),
         scratch_shapes=[
+            pltpu.VMEM((words, columns), jnp.int32),
+            pltpu.VMEM((K, words * BITS), jnp.bfloat16),
+            pltpu.VMEM((2, columns), jnp.int32),
+            pltpu.VMEM((pieces, PIECE), jnp.int32),
             pltpu.VMEM((K, depth), jnp.bfloat16),
             pltpu.VMEM((pieces, K, PIECE), jnp.float32),
             pltpu.VMEM((pieces, K, PIECE), jnp.float32),
@@ -267,6 +306,7 @@
             pltpu.VMEM((plane_size, 1, 2 * K), jnp.float32),
             pltpu.VMEM((planes, 1, 2 * K), jnp.float32),
             dma, dma, dma, dma, dma((2,)), dma((2,)), dma, dma, dma, dma,
+            dma((pieces // 2,)), dma((3,)), pltpu.SemaphoreType.REGULAR((3,)),
         ],
         compiler_params=pltpu.CompilerParams(collective_id=0, has_side_effects=True),
     )(packed_panel, components, bounds, band_width.reshape(pieces, PIECE))

time: 37.4 us -> 34.5 us (0.922)
  Pallas kernels: 35.9 us -> 33.1 us
    pallas_call x1, Pallas kernels: 35.9 us -> 33.1 us  [on_device(): pl.pallas_call(functools.partial(kernel, haps, snps), out_shape=jax.Shape...]
where the time goes in v2:
time: 34.5 us; the launch traced here: 34.3 us
  Pallas kernels  33.1 us (96%)
  local copies, waits for them, and re-layouts  1.28 us (4%)
    pallas_call x1, Pallas kernels, on_device(): pl.pallas_call(functools.partial(kernel, haps, snps), out_shape=jax.Shape...  33.1 us
    unnamed x1, local copies, waits for them, and re-layouts  1.28 us

profile of v2, /device:TPU:1, one launch (start us, length us, event | category | flops | bytes accessed | tf_op | source)
XLA Modules:
  0.0 34.3 jit_solution(12532013455444910219)
XLA Ops:
  0.0 33.1 %shard_map.46 = f32[8,128]{1,0:T(8,128)} custom-call(s32[48,1024]{1,0:T(8,128)} %panel_in.1, bf16[64,624]{1,0:T(8,128)(2,1)} %comp_in.1, s32[2,1024]{1,0:T(2,128)} %bounds_in.1, s32[8,128]{1,0:T(8,128)} %bitcast.3), custom_call_target="tpu_custom_call" | custom-call | tf_op jit(solution)/shard_map/pallas_call | solution.py:288
  33.1 1.3 %copy.6 = f32[1024]{0:T(1024)} copy(f32[1024]{0:T(1024)} %bitcast.2) | data formatting | bytes 8192
